TPU v7x, 32 devices: a whole 2x2x4 slice. The times are simulated.
32 devices in a mesh: ep: 4 (over y, x), tp: 4 (over z), dp: 2 (over core).
Axes of the slice: x: 2, y: 2, z: 4, core: 2. Of those that a mesh axis runs over, the one named last changes fastest.
Arguments:
- down_weight: bfloat16 [4, 16384, 3072], P('ep', 'tp', 'dp'), may hold values from -130 to 130
- owned_span: int32 [4, 4, 2], replicated, may hold values from 0 to 31, as said below
Outputs:
- saved_spans: bfloat16 [4, 4, 768, 16384], P('ep', 'tp', 'dp')
Inputs may be any that keep to these rules, and one draw needn't show every extreme that they name: `owned_span`: block g holds rows (g % 8) * 384 onward of expert g // 8; every block is stored by exactly one device; the block at [i, j, k] has (g % 8) // 4 == k; for each k the experts of the stored blocks form a Latin square over i and j: each expert once for each i and once for each j.
All inputs are finite; a program needn't handle non-finite values.
Results may differ from a plain program's by a relative error of at most 0.001.
Values may be sent and summed in bfloat16 or wider, within the bound.
A program may use at most 128 MiB of HBM per device.

v0:
```python
import functools

import jax
import jax.numpy as jnp
from jax import lax
from jax.experimental import pallas as pl
from jax.experimental.pallas import tpu as pltpu
from jax.sharding import PartitionSpec as P

MESH = pl.DeviceIdType.MESH
LANES = 128
SUBLANES = 16
CHUNK = 256
STAGES = 4
AHEAD = 2
SPARE = 3 << 20
WRITES = 8


def pick(values, index):
    chosen = values[0]
    for b in range(1, len(values)):
        chosen = jnp.where(index == b, values[b], chosen)
    return chosen


def kernel(n_ep, n_tp, n_dp, chunk, weight, span, out, stage, turned, send, relay,
           load_sem, ep_send, ep_recv, tp_send, tp_recv, own_sem, *arrived):
    my_ep = lax.axis_index("ep")
    my_tp = lax.axis_index("tp")
    my_dp = lax.axis_index("dp")
    hidden, width = weight.shape[1], weight.shape[2]
    rows = width // n_tp
    chunks = hidden // chunk
    per_expert = n_tp * n_dp

    def load(c):
        return pltpu.make_async_copy(
            weight.at[0, pl.ds(c * chunk, chunk)], stage.at[c % STAGES], load_sem.at[c % STAGES])

    def to_ep(c, d):
        return pltpu.make_async_remote_copy(
            send.at[c, d], arrived[c].at[d], ep_send.at[c, d], ep_recv.at[c, d],
            device_id={"ep": lax.rem(my_ep + d, n_ep)}, device_id_type=MESH)

    def columns(tp, c):
        return out.at[0, 0, :, pl.ds(pl.multiple_of(tp * hidden + c * chunk, chunk), chunk)]

    def to_tp(c, d):
        return pltpu.make_async_remote_copy(
            relay.at[c, d], columns(my_tp, c), tp_send.at[c, d], tp_recv.at[c, d],
            device_id={"tp": lax.rem(my_tp + d, n_tp)}, device_id_type=MESH)

    def from_tp(c, d):
        return pltpu.make_async_remote_copy(
            relay.at[c, d], columns(lax.rem(my_tp + n_tp - d, n_tp), c), tp_send.at[c, d], tp_recv.at[c, d],
            device_id={"tp": lax.rem(my_tp + d, n_tp)}, device_id_type=MESH)

    def own(c):
        return pltpu.make_async_copy(relay.at[c, 0], columns(my_tp, c), own_sem.at[c])

    for c in range(min(STAGES, chunks)):
        load(c).start()

    barrier = pltpu.get_barrier_semaphore()
    for d in range(1, n_ep):
        pl.semaphore_signal(barrier, inc=1, device_id={"ep": lax.rem(my_ep + d, n_ep)}, device_id_type=MESH)
    for d in range(1, n_tp):
        pl.semaphore_signal(barrier, inc=1, device_id={"tp": lax.rem(my_tp + d, n_tp)}, device_id_type=MESH)

    wanted = []
    for d in range(n_ep):
        i = lax.rem(my_ep + d, n_ep)
        total = jnp.int32(0)
        for j in range(n_tp):
            g = span[i, my_dp, j]
            total = total + jnp.where(g // per_expert == my_ep, g % per_expert - my_dp * n_tp, 0)
        wanted.append(total)
    slot = []
    for d in range(n_tp):
        j = lax.rem(my_tp + d, n_tp)
        slot.append(lax.rem(my_ep + n_ep - span[my_ep, my_dp, j] // per_expert, n_ep))

    def first_half(c):
        load(c).wait()

        @pl.loop(0, width // LANES)
        def _(b):
            at = pl.multiple_of(b * LANES, LANES)
            turned[pl.ds(at, LANES), :] = stage[c % STAGES, :, pl.ds(at, LANES)].T

        if c == 0:
            pl.semaphore_wait(barrier, n_ep + n_tp - 2)
        if c + STAGES < chunks:
            load(c + STAGES).start()
        for d in range(n_ep - 1, -1, -1):
            block = pick([turned[b * rows:(b + 1) * rows, :] for b in range(n_tp)], wanted[d])
            if d == 0:
                arrived[c][0] = block
            else:
                send[c, d] = block
                to_ep(c, d).start()

    def second_half(c):
        for d in range(1, n_ep):
            to_ep(c, d).wait_recv()
        for d in range(n_tp - 1, -1, -1):
            relay[c, d] = pick([arrived[c][s] for s in range(n_ep)], slot[d])
            if d == 0:
                own(c).start()
            else:
                to_tp(c, d).start()

    for step in range(chunks + AHEAD):
        if step < chunks:
            first_half(step)
        if step >= AHEAD:
            second_half(step - AHEAD)

    for c in range(chunks):
        for d in range(1, n_ep):
            to_ep(c, d).wait_send()
        for d in range(1, n_tp):
            from_tp(c, d).wait_recv()
            to_tp(c, d).wait_send()
        own(c).wait()


def writer(saved, out, sem):
    pieces = sem.shape[0]
    rows = saved.shape[2] // pieces
    copies = [
        pltpu.make_async_copy(
            saved.at[0, 0, pl.ds(p * rows, rows)], out.at[0, 0, pl.ds(p * rows, rows)], sem.at[p])
        for p in range(pieces)
    ]
    for copy in copies:
        copy.start()
    for copy in copies:
        copy.wait()


def write_out(saved):
    tiles = max(saved.shape[2] // SUBLANES, 1)
    pieces = max(p for p in range(1, WRITES + 1) if tiles % p == 0)
    return pl.pallas_call(
        writer,
        out_shape=jax.ShapeDtypeStruct(saved.shape, saved.dtype),
        in_specs=[pl.BlockSpec(memory_space=pltpu.VMEM)],
        out_specs=pl.BlockSpec(memory_space=pl.ANY),
        scratch_shapes=[pltpu.SemaphoreType.DMA((pieces,))],
        compiler_params=pltpu.CompilerParams(vmem_limit_bytes=SPARE),
    )(saved)


def local(down_weight, owned_span):
    n_ep, n_tp, n_dp = (lax.axis_size(a) for a in ("ep", "tp", "dp"))
    _, hidden, width = down_weight.shape
    rows = width // n_tp
    chunk = min(CHUNK, hidden)
    chunks = hidden // chunk
    kind = down_weight.dtype
    block = rows * chunk * kind.itemsize
    scratch_bytes = (STAGES + 1) * n_tp * block + chunks * (2 * n_ep + n_tp) * block
    saved = pl.pallas_call(
        functools.partial(kernel, n_ep, n_tp, n_dp, chunk),
        out_shape=pltpu.VMEM((1, 1, rows, n_tp * hidden), kind),
        in_specs=[pl.BlockSpec(memory_space=pl.ANY), pl.BlockSpec(memory_space=pltpu.SMEM)],
        out_specs=pl.BlockSpec(memory_space=pltpu.VMEM),
        scratch_shapes=[
            pltpu.VMEM((STAGES, chunk, width), kind),
            pltpu.VMEM((width, chunk), kind),
            pltpu.VMEM((chunks, n_ep, rows, chunk), kind),
            pltpu.VMEM((chunks, n_tp, rows, chunk), kind),
            pltpu.SemaphoreType.DMA((STAGES,)),
            pltpu.SemaphoreType.DMA((chunks, n_ep)),
            pltpu.SemaphoreType.DMA((chunks, n_ep)),
            pltpu.SemaphoreType.DMA((chunks, n_tp)),
            pltpu.SemaphoreType.DMA((chunks, n_tp)),
            pltpu.SemaphoreType.DMA((chunks,)),
        ] + [pltpu.VMEM((n_ep, rows, chunk), kind) for _ in range(chunks)],
        compiler_params=pltpu.CompilerParams(
            collective_id=0, has_side_effects=True, vmem_limit_bytes=scratch_bytes + SPARE),
    )(down_weight, jnp.transpose(owned_span, (0, 2, 1)))
    return write_out(saved)


def solution(mesh):
    return jax.shard_map(
        local,
        mesh=mesh,
        in_specs=(P("ep", "tp", "dp"), P()),
        out_specs=P("ep", "tp", "dp", None),
        check_vma=False,
    )
```

profile of v0, /device:TPU:0, one launch (start us, length us, event | category | flops | bytes accessed | tf_op | source)
XLA Modules:
  0.0 295.4 jit_solution(14179840236495436397)
XLA Ops:
  0.0 290.7 %shard_map.28.saved = bf16[1,1,384,16384]{3,2,1,0:T(8,128)(2,1)S(1)} custom-call(bf16[1,4096,1536]{2,1,0:T(8,128)(2,1)} %weight.1, s32[4,2,4]{2,1,0:T(2,128)} %bitcast.1), custom_call_target="tpu_custom_call" | custom-call | tf_op jit(solution)/shard_map/pallas_call | solution.py:165
  290.7 4.7 %shard_map.29 = bf16[1,1,384,16384]{3,2,1,0:T(8,128)(2,1)} custom-call(bf16[1,1,384,16384]{3,2,1,0:T(8,128)(2,1)S(1)} %shard_map.28.saved), custom_call_target="tpu_custom_call" | custom-call | tf_op jit(solution)/shard_map/pallas_call | solution.py:146
where the time goes:
time: 296 us; the launch traced here: 295 us
  Pallas kernels  295 us (100%)
    pallas_call x1, Pallas kernels, local(): pl.pallas_call(functools.partial(kernel, n_ep, n_tp, n_dp, chunk), out_sh...  291 us

commit v1 on v0

--- a/solution.py
+++ b/solution.py
@@ -25,7 +25,8 @@
 
 
 def kernel(n_ep, n_tp, n_dp, chunk, weight, span, out, stage, turned, send, relay,
-           load_sem, ep_send, ep_recv, tp_send, tp_recv, own_sem, *arrived):
+           load_sem, ep_send, ep_recv, tp_send, tp_recv, own_sem, early, middle, spread, late,
+           early_send, early_recv, fan_send, fan_recv, late_sem, *arrived):
     my_ep = lax.axis_index("ep")
     my_tp = lax.axis_index("tp")
     my_dp = lax.axis_index("dp")
@@ -40,7 +41,7 @@
 
     def to_ep(c, d):
         return pltpu.make_async_remote_copy(
-            send.at[c, d], arrived[c].at[d], ep_send.at[c, d], ep_recv.at[c, d],
+            send.at[c, d], arrived[c - 1].at[d], ep_send.at[c, d], ep_recv.at[c, d],
             device_id={"ep": lax.rem(my_ep + d, n_ep)}, device_id_type=MESH)
 
     def columns(tp, c):
@@ -58,6 +59,19 @@
 
     def own(c):
         return pltpu.make_async_copy(relay.at[c, 0], columns(my_tp, c), own_sem.at[c])
+
+    def early_to_tp(d):
+        return pltpu.make_async_remote_copy(
+            early.at[d - 1], middle.at[d], early_send.at[d], early_recv.at[d],
+            device_id={"tp": lax.rem(my_tp + d, n_tp)}, device_id_type=MESH)
+
+    def fan(d):
+        return pltpu.make_async_remote_copy(
+            middle, spread.at[d - 1], fan_send.at[d], fan_recv.at[d],
+            device_id={"ep": lax.rem(my_ep + d, n_ep)}, device_id_type=MESH)
+
+    def late_own(p):
+        return pltpu.make_async_copy(late.at[p], columns(lax.rem(my_tp + n_tp - p, n_tp), 0), late_sem.at[p])
 
     for c in range(min(STAGES, chunks)):
         load(c).start()
@@ -81,7 +95,16 @@
         j = lax.rem(my_tp + d, n_tp)
         slot.append(lax.rem(my_ep + n_ep - span[my_ep, my_dp, j] // per_expert, n_ep))
 
-    def first_half(c):
+    sooner = []
+    for d in range(n_tp):
+        j = lax.rem(my_tp + d, n_tp)
+        total = jnp.int32(0)
+        for i in range(n_ep):
+            g = span[i, my_dp, j]
+            total = total + jnp.where(g // per_expert == my_ep, g % per_expert - my_dp * n_tp, 0)
+        sooner.append(total)
+
+    def turn(c):
         load(c).wait()
 
         @pl.loop(0, width // LANES)
@@ -89,41 +112,69 @@
             at = pl.multiple_of(b * LANES, LANES)
             turned[pl.ds(at, LANES), :] = stage[c % STAGES, :, pl.ds(at, LANES)].T
 
-        if c == 0:
-            pl.semaphore_wait(barrier, n_ep + n_tp - 2)
         if c + STAGES < chunks:
             load(c + STAGES).start()
+
+    def block_of(index):
+        return pick([turned[b * rows:(b + 1) * rows, :] for b in range(n_tp)], index)
+
+    def first_half(c):
+        turn(c)
         for d in range(n_ep - 1, -1, -1):
-            block = pick([turned[b * rows:(b + 1) * rows, :] for b in range(n_tp)], wanted[d])
             if d == 0:
-                arrived[c][0] = block
+                arrived[c - 1][0] = block_of(wanted[d])
             else:
-                send[c, d] = block
+                send[c, d] = block_of(wanted[d])
                 to_ep(c, d).start()
 
     def second_half(c):
         for d in range(1, n_ep):
             to_ep(c, d).wait_recv()
         for d in range(n_tp - 1, -1, -1):
-            relay[c, d] = pick([arrived[c][s] for s in range(n_ep)], slot[d])
+            relay[c, d] = pick([arrived[c - 1][s] for s in range(n_ep)], slot[d])
             if d == 0:
                 own(c).start()
             else:
                 to_tp(c, d).start()
 
-    for step in range(chunks + AHEAD):
+    turn(0)
+    for d in range(1, n_tp):
+        early[d - 1] = block_of(sooner[d])
+        if d == 1:
+            pl.semaphore_wait(barrier, n_ep + n_tp - 2)
+        early_to_tp(d).start()
+    middle[0] = block_of(sooner[0])
+
+    for step in range(1, chunks + AHEAD):
         if step < chunks:
             first_half(step)
-        if step >= AHEAD:
+        if step == chunks:
+            for d in range(1, n_tp):
+                early_to_tp(d).wait_recv()
+            for d in range(1, n_ep):
+                fan(d).start()
+        if step > AHEAD:
             second_half(step - AHEAD)
 
-    for c in range(chunks):
+    for d in range(1, n_ep):
+        fan(d).wait_recv()
+    for p in range(n_tp):
+        late[p] = pick([middle[p]] + [spread[d - 1, p] for d in range(1, n_ep)], slot[0])
+        late_own(p).start()
+
+    for d in range(1, n_ep):
+        fan(d).wait_send()
+    for d in range(1, n_tp):
+        early_to_tp(d).wait_send()
+    for c in range(1, chunks):
         for d in range(1, n_ep):
             to_ep(c, d).wait_send()
         for d in range(1, n_tp):
             from_tp(c, d).wait_recv()
             to_tp(c, d).wait_send()
         own(c).wait()
+    for p in range(n_tp):
+        late_own(p).wait()
 
 
 def writer(saved, out, sem):
@@ -161,7 +212,7 @@
     chunks = hidden // chunk
     kind = down_weight.dtype
     block = rows * chunk * kind.itemsize
-    scratch_bytes = (STAGES + 1) * n_tp * block + chunks * (2 * n_ep + n_tp) * block
+    scratch_bytes = (STAGES + 1) * n_tp * block + chunks * (2 * n_ep + n_tp) * block + (n_ep + 2) * n_tp * block
     saved = pl.pallas_call(
         functools.partial(kernel, n_ep, n_tp, n_dp, chunk),
         out_shape=pltpu.VMEM((1, 1, rows, n_tp * hidden), kind),
@@ -178,7 +229,16 @@
             pltpu.SemaphoreType.DMA((chunks, n_tp)),
             pltpu.SemaphoreType.DMA((chunks, n_tp)),
             pltpu.SemaphoreType.DMA((chunks,)),
-        ] + [pltpu.VMEM((n_ep, rows, chunk), kind) for _ in range(chunks)],
+                    pltpu.VMEM((n_tp - 1, rows, chunk), kind),
+            pltpu.VMEM((n_tp, rows, chunk), kind),
+            pltpu.VMEM((n_ep - 1, n_tp, rows, chunk), kind),
+            pltpu.VMEM((n_tp, rows, chunk), kind),
+            pltpu.SemaphoreType.DMA((n_tp,)),
+            pltpu.SemaphoreType.DMA((n_tp,)),
+            pltpu.SemaphoreType.DMA((n_ep,)),
+            pltpu.SemaphoreType.DMA((n_ep,)),
+            pltpu.SemaphoreType.DMA((n_tp,)),
+        ] + [pltpu.VMEM((n_ep, rows, chunk), kind) for _ in range(chunks - 1)],
         compiler_params=pltpu.CompilerParams(
             collective_id=0, has_side_effects=True, vmem_limit_bytes=scratch_bytes + SPARE),
     )(down_weight, jnp.transpose(owned_span, (0, 2, 1)))

time: 296 us -> 285 us (0.963)
  Pallas kernels: 295 us -> 285 us
    pallas_call x1, Pallas kernels: 291 us -> 280 us  [local(): pl.pallas_call(functools.partial(kernel, n_ep, n_tp, n_dp, chunk), out_sh...]
where the time goes in v1:
time: 285 us
  Pallas kernels  285 us (100%)
    pallas_call x1, Pallas kernels, local(): pl.pallas_call(functools.partial(kernel, n_ep, n_tp, n_dp, chunk), out_sh...  280 us

profile of v1, /device:TPU:0, one launch (start us, length us, event | category | flops | bytes accessed | tf_op | source)
XLA Modules:
  0.0 284.9 jit_solution(11664296567735106844)
XLA Ops:
  0.0 280.2 %shard_map.28.saved = bf16[1,1,384,16384]{3,2,1,0:T(8,128)(2,1)S(1)} custom-call(bf16[1,4096,1536]{2,1,0:T(8,128)(2,1)} %weight.1, s32[4,2,4]{2,1,0:T(2,128)} %bitcast.1), custom_call_target="tpu_custom_call" | custom-call | tf_op jit(solution)/shard_map/pallas_call | solution.py:216
  280.2 4.7 %shard_map.29 = bf16[1,1,384,16384]{3,2,1,0:T(8,128)(2,1)} custom-call(bf16[1,1,384,16384]{3,2,1,0:T(8,128)(2,1)S(1)} %shard_map.28.saved), custom_call_target="tpu_custom_call" | custom-call | tf_op jit(solution)/shard_map/pallas_call | solution.py:197

commit v2 on v1

--- a/solution.py
+++ b/solution.py
@@ -73,8 +73,7 @@
     def late_own(p):
         return pltpu.make_async_copy(late.at[p], columns(lax.rem(my_tp + n_tp - p, n_tp), 0), late_sem.at[p])
 
-    for c in range(min(STAGES, chunks)):
-        load(c).start()
+    load(0).start()
 
     barrier = pltpu.get_barrier_semaphore()
     for d in range(1, n_ep):
@@ -106,6 +105,9 @@
 
     def turn(c):
         load(c).wait()
+        if c == 0:
+            for later in range(1, min(STAGES, chunks)):
+                load(later).start()
 
         @pl.loop(0, width // LANES)
         def _(b):
@@ -130,12 +132,13 @@
     def second_half(c):
         for d in range(1, n_ep):
             to_ep(c, d).wait_recv()
-        for d in range(n_tp - 1, -1, -1):
-            relay[c, d] = pick([arrived[c - 1][s] for s in range(n_ep)], slot[d])
-            if d == 0:
-                own(c).start()
-            else:
-                to_tp(c, d).start()
+        for k in range(1, n_tp):
+            d = jnp.where(my_tp < n_tp // 2, k, n_tp - k)
+            index = jnp.where(my_tp < n_tp // 2, slot[k], slot[n_tp - k])
+            relay[c, d] = pick([arrived[c - 1][s] for s in range(n_ep)], index)
+            to_tp(c, d).start()
+        relay[c, 0] = pick([arrived[c - 1][s] for s in range(n_ep)], slot[0])
+        own(c).start()
 
     turn(0)
     for d in range(1, n_tp):

time: 285 us -> 285 us (level)
  no operation moved by 1% of the time
where the time goes in v2:
time: 285 us
  Pallas kernels  285 us (100%)
    pallas_call x1, Pallas kernels, local(): pl.pallas_call(functools.partial(kernel, n_ep, n_tp, n_dp, chunk), out_sh...  280 us

profile of v2, /device:TPU:0, one launch (start us, length us, event | category | flops | bytes accessed | tf_op | source)
XLA Modules:
  0.0 284.9 jit_solution(17033538026523695729)
XLA Ops:
  0.0 280.2 %shard_map.28.saved = bf16[1,1,384,16384]{3,2,1,0:T(8,128)(2,1)S(1)} custom-call(bf16[1,4096,1536]{2,1,0:T(8,128)(2,1)} %weight.1, s32[4,2,4]{2,1,0:T(2,128)} %bitcast.1), custom_call_target="tpu_custom_call" | custom-call | tf_op jit(solution)/shard_map/pallas_call | solution.py:219
  280.2 4.7 %shard_map.29 = bf16[1,1,384,16384]{3,2,1,0:T(8,128)(2,1)} custom-call(bf16[1,1,384,16384]{3,2,1,0:T(8,128)(2,1)S(1)} %shard_map.28.saved), custom_call_target="tpu_custom_call" | custom-call | tf_op jit(solution)/shard_map/pallas_call | solution.py:200
